TPU v7x, 32 devices: a whole 2x2x4 slice. The times are simulated.
32 devices in a mesh: atoms: 8 (over y, x, core), gsplit: 4 (over z).
Axes of the slice: x: 2, y: 2, z: 4, core: 2. Of those that a mesh axis runs over, the one named last changes fastest.
Arguments:
- miller: int32 [3, 30720], P(None, 'gsplit'), may hold values from -16 to 16, as said below
- form_factors: bfloat16 [49, 30720], P(None, 'gsplit'), may hold values from -6 to 6
- fractional: float32 [3, 512], P(None, 'atoms'), may hold values from 0 to 1
- multipoles: bfloat16 [2, 49, 512], P(None, None, 'atoms'), may hold values from -0.0390625 to 0.0390625
- point_owner: int32 [1024], P(('atoms', 'gsplit')), may hold values from 0 to 63
- offsets: float32 [3, 1024], P(None, ('atoms', 'gsplit')), may hold values from -0.05 to 0.05
Outputs:
- grid_potential: float32 [2, 1024], P(None, ('atoms', 'gsplit'))
- moments: float32 [2, 49, 512], P(None, None, ('atoms', 'gsplit'))
Inputs may be any that keep to these rules, and one draw needn't show every extreme that they name: `miller`: no vector has all three indices zero. Point p belongs to atom (p // 128) * 64 + point_owner[p].
All inputs are finite; a program needn't handle non-finite values.
Results may differ from a plain program's by a relative error of at most 0.0045.
Values may be sent and summed in bfloat16 or wider, within the bound.
A program may use at most 64 MiB of HBM per device.

v0:
```python
import math
import jax
import jax.numpy as jnp
from jax import lax
from jax.sharding import PartitionSpec as P

two_pi = 2.0 * math.pi
damping = 1.0 / 400.0


def angles(vectors, places):
    indices = vectors.astype(jnp.float32)
    summed = (
        places[0][:, None] * indices[0][None, :]
        + places[1][:, None] * indices[1][None, :]
        + places[2][:, None] * indices[2][None, :]
    )
    return two_pi * summed


def sign_tables(comp_count):
    comp_ids = jnp.arange(comp_count, dtype=jnp.int32)
    degree = jnp.zeros((comp_count,), jnp.int32)
    for degree_step in range(1, 16):
        degree = degree + (comp_ids >= degree_step * degree_step).astype(jnp.int32)
    quarter = degree % 4
    even_sign = jnp.where(quarter == 0, 1.0, jnp.where(quarter == 2, -1.0, 0.0)).astype(jnp.float32)
    odd_sign = jnp.where(quarter == 3, 1.0, jnp.where(quarter == 1, -1.0, 0.0)).astype(jnp.float32)
    return (even_sign, odd_sign)


def coulomb(vectors):
    indices = vectors.astype(jnp.float32)
    square = indices[0] * indices[0] + indices[1] * indices[1] + indices[2] * indices[2]
    return jnp.exp(-damping * square) / square


def structure(multipoles, cos_table, sin_table, form_block, even_sign, odd_sign):
    density_count, comp_count, atom_count = multipoles.shape
    flattened = multipoles.reshape(density_count * comp_count, atom_count)
    along_cos = jnp.dot(flattened, cos_table, preferred_element_type=jnp.float32).reshape(
        density_count, comp_count, -1
    )
    along_sin = jnp.dot(flattened, sin_table, preferred_element_type=jnp.float32).reshape(
        density_count, comp_count, -1
    )
    weights = form_block.astype(jnp.float32)[None]
    even_wide = even_sign[None, :, None]
    odd_wide = odd_sign[None, :, None]
    real_part = jnp.sum(weights * (even_wide * along_cos + odd_wide * along_sin), axis=1)
    imag_part = jnp.sum(weights * (odd_wide * along_cos - even_wide * along_sin), axis=1)
    return jnp.stack([real_part, imag_part], axis=1)


def moment_terms(potential, form_block, cos_table, sin_table, even_sign, odd_sign):
    weighted = (form_block.astype(jnp.float32)[None, None] * potential[:, :, None, :]).astype(
        jnp.bfloat16
    )
    density_count, _, comp_count, vector_count = weighted.shape
    even_rows = (even_sign != 0.0)[None, :, None]
    against_cos = jnp.where(even_rows, weighted[:, 0], weighted[:, 1]).reshape(
        density_count * comp_count, vector_count
    )
    against_sin = jnp.where(even_rows, weighted[:, 1], weighted[:, 0]).reshape(
        density_count * comp_count, vector_count
    )
    contract = (((1,), (1,)), ((), ()))
    with_cos = lax.dot_general(
        against_cos, cos_table, contract, preferred_element_type=jnp.float32
    ).reshape(density_count, comp_count, -1)
    with_sin = lax.dot_general(
        against_sin, sin_table, contract, preferred_element_type=jnp.float32
    ).reshape(density_count, comp_count, -1)
    even_wide = even_sign[None, :, None]
    odd_wide = odd_sign[None, :, None]
    return even_wide * (with_cos - with_sin) + odd_wide * (with_cos + with_sin)


def grid_rows(rounded, vectors, places):
    point_angles = angles(vectors, places)
    cos_points = jnp.cos(point_angles).astype(jnp.bfloat16)
    sin_points = jnp.sin(point_angles).astype(jnp.bfloat16)
    contract = (((1,), (1,)), ((), ()))
    return lax.dot_general(
        cos_points, rounded[:, 0], contract, preferred_element_type=jnp.float32
    ) - lax.dot_general(sin_points, rounded[:, 1], contract, preferred_element_type=jnp.float32)


def grid_blocked(rounded, vectors, places):
    point_count = places.shape[1]
    return grid_rows(rounded, vectors, places)


def shards(miller, form_factors, fractional, multipoles, point_owner, offsets):
    even_sign, odd_sign = sign_tables(form_factors.shape[0])
    phases = angles(miller, fractional)
    cos_table = jnp.cos(phases).astype(jnp.bfloat16)
    sin_table = jnp.sin(phases).astype(jnp.bfloat16)
    partial_sums = structure(multipoles, cos_table, sin_table, form_factors, even_sign, odd_sign)
    summed = lax.psum(partial_sums, "atoms")
    potential = coulomb(miller)[None, None, :] * summed
    local_moments = moment_terms(potential, form_factors, cos_table, sin_table, even_sign, odd_sign)
    moments = lax.psum_scatter(local_moments, "gsplit", scatter_dimension=2, tiled=True)
    atom_ids = jnp.arange(fractional.shape[1], dtype=jnp.int32)
    onehot = (atom_ids[:, None] == point_owner[None, :]).astype(jnp.float32)
    places = (
        jnp.dot(
            fractional, onehot, precision=lax.Precision.HIGHEST, preferred_element_type=jnp.float32
        )
        + offsets
    )
    rounded = potential.astype(jnp.bfloat16)
    every_vector = lax.all_gather(miller, "gsplit", axis=1, tiled=True)
    every_potential = lax.all_gather(rounded, "gsplit", axis=2, tiled=True)
    point_rows = grid_blocked(every_potential, every_vector, places)
    return (point_rows.T, moments)


def solution(mesh):
    placed = (
        P(None, "gsplit"),
        P(None, "gsplit"),
        P(None, "atoms"),
        P(None, None, "atoms"),
        P(("atoms", "gsplit")),
        P(None, ("atoms", "gsplit")),
    )
    return jax.shard_map(
        shards,
        mesh=mesh,
        in_specs=placed,
        out_specs=(P(None, ("atoms", "gsplit")), P(None, None, ("atoms", "gsplit"))),
        check_vma=False,
    )
```

profile of v0, /device:TPU:0, one launch (start us, length us, event | category | flops | bytes accessed | tf_op | source)
XLA Modules:
  0.0 180.9 jit_solution(15231726801209480579)
XLA Ops:
  7.2 0.9 convert_element_type.435
  8.1 0.2 slice_reduce_fusion.2
  8.4 0.8 slice_bitcast_fusion.15
  9.2 0.8 copy.11
  10.1 8.7 %convolution_bitcast_fusion.1 = f32[98,7680]{1,0:T(8,128)} fusion(bf16[98,64]{0,1:T(8,128)(2,1)S(1)} %reshape.154, f32[7680]{0:T(1024)S(1)} %get-tuple-element.11, f32[64]{0:T(128)S(1)} %get-tuple-element.20, f32[7680]{0:T(1024)S(1)} %get-tuple-element.12, f32[64]{0:T(128)S(1)} %get-tuple-element.19, f32[7680]{0:T(1024)S(1)} %get-tuple-element.10, ...), kind=kOutput, calls=%fused_computation.1 | convolution fusion | flops 99778560 | bytes 3116032 | tf_op jit(solution)/shard_map/dot_general | solution.py:41
  18.8 7.0 %convolution_bitcast_fusion = f32[98,7680]{1,0:T(8,128)S(1)} fusion(bf16[98,64]{0,1:T(8,128)(2,1)S(1)} %reshape.154, f32[7680]{0:T(1024)S(1)} %get-tuple-element.11, f32[64]{0:T(128)S(1)} %get-tuple-element.20, f32[7680]{0:T(1024)S(1)} %get-tuple-element.12, f32[64]{0:T(128)S(1)} %get-tuple-element.19, f32[7680]{0:T(1024)S(1)} %get-tuple-element.10, ...), kind=kOutput, calls=%fused_computation | convolution fusion | flops 99778560 | bytes 3116032 | tf_op jit(solution)/shard_map/dot_general | solution.py:44
  25.9 4.0 %reshape.155 = f32[2,49,7680]{2,1,0:T(8,128)} reshape(f32[98,7680]{1,0:T(8,128)} %convolution_bitcast_fusion.1) | data formatting | bytes 6021120 | tf_op jit(solution)/shard_map/reshape | solution.py:41
  29.8 2.1 %reshape.156 = f32[2,49,7680]{2,1,0:T(8,128)} reshape(f32[98,7680]{1,0:T(8,128)S(1)} %convolution_bitcast_fusion) | data formatting | bytes 6021120 | tf_op jit(solution)/shard_map/reshape | solution.py:44
  31.9 1.3 convert_element_type.436
  33.2 4.5 %multiply_reduce_fusion.1 = (f32[2,7680]{1,0:T(2,128)S(1)}, f32[2,7680]{1,0:T(2,128)S(1)}) fusion(f32[2,49,7680]{2,1,0:T(8,128)} %reshape.156, f32[2,49,7680]{2,1,0:T(8,128)} %reshape.155, f32[49]{0:T(128)S(1)} %get-tuple-element.24, f32[49]{0:T(128)S(1)} %get-tuple-element.25, f32[49,7680]{1,0:T(8,128)S(1)} %convert_element_type.436), kind=kLoop, calls=%fused_computation.7 | loop fusion | flops 7495680 | bytes 7649672 | tf_op jit(solution)/shard_map/reduce_sum | solution.py:50
  37.8 0.7 pad_maximum_fusion
  38.6 17.6 %all_gather.7 = s32[3,30720]{1,0:T(4,128)S(1)} all-gather(s32[3,7680]{1,0:T(4,128)S(1)} %copy-done), channel_id=1, replica_groups=mesh['atoms'=8,'gsplit'=4] {'gsplit'}, dimensions={1}, use_global_device_ids=true | all-gather | bytes 460800 | tf_op jit(solution)/shard_map/all_gather | solution.py:113
  56.2 0.3 fusion.54
  56.7 0.6 dynamic-slice
  57.9 36.2 %all-reduce.3.cloned.1.call-done = f32[2,2,7680]{2,0,1:T(2,128)} async-done(((f32[2,2,7680]{2,0,1:T(2,128)}), f32[2,2,7680]{2,0,1:T(2,128)}) %all-reduce.3.cloned.1.call-update) | async-done | bytes 122896 | tf_op jit(solution)/shard_map/psum | solution.py:100
  94.1 1.0 fusion.53
  95.1 0.4 multiply_convert_fusion
  95.5 7.4 %fusion.2 = f32[2,49,64]{2,1,0:T(8,128)S(1)} fusion(pred[49]{0:T(512)(128)(4,1)S(1)} %broadcast_compare_fusion, bf16[2,2,49,7680]{3,2,0,1:T(8,128)(2,1)S(1)} %multiply_convert_fusion, f32[7680]{0:T(1024)S(1)} %get-tuple-element.11, f32[64]{0:T(128)S(1)} %get-tuple-element.20, f32[7680]{0:T(1024)S(1)} %get-tuple-element.12, f32[64]{0:T(128)S(1)} %get-tuple-element.19, ...), kind=kOutput, calls=%fused_computation.15 | convolution fusion | flops 100531200 | bytes 3128625 | tf_op jit(solution)/shard_map/dot_general | solution.py:71
  102.9 7.5 %multiply_add_fusion = f32[2,49,64]{2,1,0:T(8,128)S(1)} fusion(f32[2,49,64]{2,1,0:T(8,128)S(1)} %fusion.2, f32[7680]{0:T(1024)S(1)} %get-tuple-element.11, f32[64]{0:T(128)S(1)} %get-tuple-element.20, f32[7680]{0:T(1024)S(1)} %get-tuple-element.12, f32[64]{0:T(128)S(1)} %get-tuple-element.19, f32[7680]{0:T(1024)S(1)} %get-tuple-element.10, ...), kind=kOutput, calls=%fused_computation.30 | convolution fusion | flops 100562560 | bytes 3154105 | tf_op jit(solution)/shard_map/dot_general | solution.py:68
  110.6 19.9 %all-reduce = f32[2,49,64]{1,0,2:T(2,128)S(1)} all-reduce(f32[2,49,64]{1,0,2:T(2,128)S(1)} %copy.12), channel_id=2, replica_groups=mesh['atoms'=8,'gsplit'=4] {'gsplit'}, use_global_device_ids=true, to_apply=%region_3.4.clone | all-reduce | flops 6272 | bytes 50176
  130.5 0.6 copy.13
  131.1 14.1 %all_gather.6 = bf16[2,2,30720]{2,0,1:T(2,128)(2,1)S(1)} all-gather(bf16[2,2,7680]{2,0,1:T(2,128)(2,1)S(1)} %get-tuple-element.13), channel_id=1, replica_groups=mesh['atoms'=8,'gsplit'=4] {'gsplit'}, dimensions={2}, use_global_device_ids=true | all-gather | bytes 307200 | tf_op jit(solution)/shard_map/all_gather | solution.py:114
  145.1 13.8 %fusion = f32[2,32]{1,0:T(2,128)S(1)} fusion(f32[30720]{0:T(1024)S(1)} %bitcast.69, f32[32]{0:T(128)S(1)} %get-tuple-element.22, f32[30720]{0:T(1024)S(1)} %bitcast.71, f32[32]{0:T(128)S(1)} %get-tuple-element.23, f32[30720]{0:T(1024)S(1)} %bitcast.67, f32[32]{0:T(128)S(1)} %get-tuple-element.21, bf16[2,2,30720]{2,0,1:T(2,128)(2,1)S(1)} %all_gather.6), kind=kOutput, calls=%fused_computation.11 | convolution fusion | flops 10813440 | bytes 493312 | tf_op jit(solution)/shard_map/dot_general | solution.py:84
  159.0 14.6 %fusion.9 = f32[2,32]{1,0:T(2,128)} fusion(f32[2,32]{1,0:T(2,128)S(1)} %fusion, f32[30720]{0:T(1024)S(1)} %bitcast.70, f32[32]{0:T(128)S(1)} %get-tuple-element.22, f32[30720]{0:T(1024)S(1)} %bitcast.72, f32[32]{0:T(128)S(1)} %get-tuple-element.23, f32[30720]{0:T(1024)S(1)} %bitcast.68, f32[32]{0:T(128)S(1)} %get-tuple-element.21, ...), kind=kOutput, calls=%fused_computation.23 | convolution fusion | flops 10813504 | bytes 494336 | tf_op jit(solution)/shard_map/dot_general | solution.py:86
  (21 shorter events, 0.6 us)
Async XLA Ops:
  7.2 87.0 %all-reduce.3.cloned.1.call-start = ((), (), s32[]{:S(2)}) async-start(), calls=%async_computation | async-start | bytes 245760 | tf_op jit(solution)/shard_map/psum | solution.py:100
  33.2 5.4 %copy-start = (s32[3,7680]{1,0:T(4,128)S(1)}, s32[3,7680]{1,0:T(4,128)}, u32[]{:S(2)}) copy-start(s32[3,7680]{1,0:T(4,128)} %param.6) | copy-start | bytes 276484
  37.7 18.7 %copy-start.1 = (f32[3,64]{1,0:T(4,128)S(1)}, f32[3,64]{1,0:T(4,128)}, u32[]{:S(2)}) copy-start(f32[3,64]{1,0:T(4,128)} %param.8) | copy-start | bytes 2308
  37.8 18.7 %copy-start.2 = (f32[3,32]{1,0:T(4,128)S(1)}, f32[3,32]{1,0:T(4,128)}, u32[]{:S(2)}) copy-start(f32[3,32]{1,0:T(4,128)} %param.11) | copy-start | bytes 1156
  37.8 18.7 %copy-start.3 = (s32[32]{0:T(128)S(1)}, s32[32]{0:T(128)}, u32[]{:S(2)}) copy-start(s32[32]{0:T(128)} %param.10) | copy-start | bytes 388
  37.8 18.9 %copy-start.4 = (u32[32]{0:T(128)S(1)}, u32[32]{0:T(128)}, u32[]{:S(2)}) copy-start(u32[32]{0:T(128)} %constant.62) | copy-start | bytes 388
Sparse Core Ops, SparseCore 0:
  38.6 55.4 all-reduce.2
where the time goes:
time: 184 us; the launch traced here: 181 us
  matrix products  59.2 us (32%)
  blocking collectives  51.5 us (28%)
  waiting for transfers between devices  36.2 us (20%)
  between operations  15.3 us (8%)
  local copies, waits for them, and re-layouts  9.62 us (5%)
  other arithmetic  8.97 us (5%)
    psum x1, waiting for transfers between devices, shards(): summed = lax.psum(partial_sums, 'atoms')  36.2 us
    unnamed x1, blocking collectives  19.9 us
    all_gather x1, blocking collectives, shards(): every_vector = lax.all_gather(miller, 'gsplit', axis=1, tiled=True)  17.6 us
    dot_general x1, matrix products, grid_rows(): lax.dot_general(sin_points, rounded[:, 1], contract, preferred_element_ty...  14.6 us
    all_gather x1, blocking collectives, shards(): every_potential = lax.all_gather(rounded, 'gsplit', axis=2, tiled=True)  14.1 us
    dot_general x1, matrix products, grid_rows(): lax.dot_general(cos_points, rounded[:, 0], contract, preferred_element_ty...  13.8 us
    dot_general x1, matrix products, structure(): jnp.dot(flattened, cos_table, preferred_element_type=jnp.float32)  8.67 us
    dot_general x1, matrix products, moment_terms(): lax.dot_general(against_cos, cos_table, contract, preferred_element_type=...  7.51 us
  transfers between devices with their start and end apart: 1, of which 1 were waited for; matrix products, arithmetic and copies ran while one was open for 1% of the time, Pallas kernels for 0%

commit v1 on v0

--- a/solution.py
+++ b/solution.py
@@ -111,7 +111,27 @@
     )
     rounded = potential.astype(jnp.bfloat16)
     every_vector = lax.all_gather(miller, "gsplit", axis=1, tiled=True)
-    every_potential = lax.all_gather(rounded, "gsplit", axis=2, tiled=True)
+
+    def list_leaves(z_in):
+        dev_n = lax.psum(1, "gsplit")
+        block_list = []
+        for rr in range(dev_n):
+            block_list.append((rr, (rr + 1) % dev_n))
+
+        def set_stocks(answer):
+            if len(answer) == dev_n:
+                return answer
+            left_arr = set_stocks([lax.ppermute(answer[0], "gsplit", block_list), *answer])
+            return left_arr
+
+        part_next = jnp.roll(
+            jnp.concatenate(set_stocks([z_in]), 2),
+            (lax.axis_index("gsplit") + 1) * z_in.shape[2],
+            2,
+        )
+        return part_next
+
+    every_potential = list_leaves(rounded)
     point_rows = grid_blocked(every_potential, every_vector, places)
     return (point_rows.T, moments)
 

time: 184 us -> 178 us (0.967)
  blocking collectives: 51.5 us -> 35.7 us
  waiting for transfers between devices: 36.2 us -> 42 us
  starting transfers between devices: 0.04 us -> 3.96 us
    all_gather x1 -> x0, blocking collectives: 14.1 us -> none  [shards(): every_potential = lax.all_gather(rounded, 'gsplit', axis=2, tiled=True)]
    ppermute x0 -> x3, waiting for transfers between devices: none -> 5.38 us  [set_stocks(): lax.ppermute(answer[0], 'gsplit', block_list)]
    ppermute x0 -> x3, starting transfers between devices: none -> 3.92 us  [set_stocks(): lax.ppermute(answer[0], 'gsplit', block_list)]
  transfers between devices with their start and end apart: 1 -> 4, of which waited for: 1 -> 2; matrix products, arithmetic and copies ran while one was open for 1% -> 9% of each run, Pallas kernels for 0% -> 0%
where the time goes in v1:
time: 178 us; the launch traced here: 175 us
  matrix products  59.2 us (33%)
  waiting for transfers between devices  42 us (24%)
  blocking collectives  35.7 us (20%)
  between operations  15.2 us (9%)
  local copies, waits for them, and re-layouts  10 us (6%)
  other arithmetic  8.97 us (5%)
  starting transfers between devices  3.96 us (2%)
    psum x1, waiting for transfers between devices, shards(): summed = lax.psum(partial_sums, 'atoms')  36.6 us
    unnamed x1, blocking collectives  18.6 us
    all_gather x1, blocking collectives, shards(): every_vector = lax.all_gather(miller, 'gsplit', axis=1, tiled=True)  17.1 us
    dot_general x1, matrix products, grid_rows(): lax.dot_general(cos_points, rounded[:, 0], contract, preferred_element_ty...  14.6 us
    dot_general x1, matrix products, grid_rows(): lax.dot_general(sin_points, rounded[:, 1], contract, preferred_element_ty...  14.1 us
    dot_general x1, matrix products, structure(): jnp.dot(flattened, cos_table, preferred_element_type=jnp.float32)  8.63 us
    dot_general x1, matrix products, moment_terms(): lax.dot_general(against_sin, sin_table, contract, preferred_element_type=...  7.4 us
    dot_general x1, matrix products, moment_terms(): lax.dot_general(against_cos, cos_table, contract, preferred_element_type=...  7.34 us
  transfers between devices with their start and end apart: 4, of which 2 were waited for; matrix products, arithmetic and copies ran while one was open for 9% of the time, Pallas kernels for 0%

profile of v1, /device:TPU:0, one launch (start us, length us, event | category | flops | bytes accessed | tf_op | source)
XLA Modules:
  0.0 175.1 jit_solution(6998674180137708004)
XLA Ops:
  7.2 0.9 convert_element_type.435
  8.4 0.8 slice_bitcast_fusion.11
  9.2 0.8 copy.11
  10.1 8.6 %convolution_bitcast_fusion.1 = f32[98,7680]{1,0:T(8,128)} fusion(bf16[98,64]{0,1:T(8,128)(2,1)S(1)} %reshape.154, f32[7680]{0:T(1024)S(1)} %get-tuple-element.11, f32[64]{0:T(128)S(1)} %get-tuple-element.20, f32[7680]{0:T(1024)S(1)} %get-tuple-element.12, f32[64]{0:T(128)S(1)} %get-tuple-element.19, f32[7680]{0:T(1024)S(1)} %get-tuple-element.10, ...), kind=kOutput, calls=%fused_computation.1 | convolution fusion | flops 99778560 | bytes 3116032 | tf_op jit(solution)/shard_map/dot_general | solution.py:41
  18.8 7.0 %convolution_bitcast_fusion = f32[98,7680]{1,0:T(8,128)S(1)} fusion(bf16[98,64]{0,1:T(8,128)(2,1)S(1)} %reshape.154, f32[7680]{0:T(1024)S(1)} %get-tuple-element.11, f32[64]{0:T(128)S(1)} %get-tuple-element.20, f32[7680]{0:T(1024)S(1)} %get-tuple-element.12, f32[64]{0:T(128)S(1)} %get-tuple-element.19, f32[7680]{0:T(1024)S(1)} %get-tuple-element.10, ...), kind=kOutput, calls=%fused_computation | convolution fusion | flops 99778560 | bytes 3116032 | tf_op jit(solution)/shard_map/dot_general | solution.py:44
  25.8 4.0 %reshape.155 = f32[2,49,7680]{2,1,0:T(8,128)} reshape(f32[98,7680]{1,0:T(8,128)} %convolution_bitcast_fusion.1) | data formatting | bytes 6021120 | tf_op jit(solution)/shard_map/reshape | solution.py:41
  29.8 2.1 %reshape.156 = f32[2,49,7680]{2,1,0:T(8,128)} reshape(f32[98,7680]{1,0:T(8,128)S(1)} %convolution_bitcast_fusion) | data formatting | bytes 6021120 | tf_op jit(solution)/shard_map/reshape | solution.py:44
  31.9 1.3 convert_element_type.436
  33.2 4.5 %multiply_reduce_fusion.1 = (f32[2,7680]{1,0:T(2,128)S(1)}, f32[2,7680]{1,0:T(2,128)S(1)}) fusion(f32[2,49,7680]{2,1,0:T(8,128)} %reshape.156, f32[2,49,7680]{2,1,0:T(8,128)} %reshape.155, f32[49]{0:T(128)S(1)} %get-tuple-element.24, f32[49]{0:T(128)S(1)} %get-tuple-element.25, f32[49,7680]{1,0:T(8,128)S(1)} %convert_element_type.436), kind=kLoop, calls=%fused_computation.7 | loop fusion | flops 7495680 | bytes 7649672 | tf_op jit(solution)/shard_map/reduce_sum | solution.py:50
  37.7 0.7 pad_maximum_fusion
  38.5 17.1 %all_gather.3 = s32[3,30720]{1,0:T(4,128)S(1)} all-gather(s32[3,7680]{1,0:T(4,128)S(1)} %copy-done), channel_id=1, replica_groups=mesh['atoms'=8,'gsplit'=4] {'gsplit'}, dimensions={1}, use_global_device_ids=true | all-gather | bytes 460800 | tf_op jit(solution)/shard_map/all_gather | solution.py:113
  56.2 0.6 dynamic-slice
  57.4 36.6 %all-reduce.3.cloned.1.call-done = f32[2,2,7680]{2,0,1:T(2,128)} async-done(((f32[2,2,7680]{2,0,1:T(2,128)}), f32[2,2,7680]{2,0,1:T(2,128)}) %all-reduce.3.cloned.1.call-update) | async-done | bytes 122896 | tf_op jit(solution)/shard_map/psum | solution.py:100
  94.1 1.0 fusion.55
  95.1 0.4 multiply_convert_fusion
  95.5 1.8 collective-permute-start
  97.2 7.4 %fusion.2 = f32[2,49,64]{2,1,0:T(8,128)S(1)} fusion(pred[49]{0:T(512)(128)(4,1)S(1)} %broadcast_compare_fusion, bf16[2,2,49,7680]{3,2,0,1:T(8,128)(2,1)S(1)} %multiply_convert_fusion, f32[7680]{0:T(1024)S(1)} %get-tuple-element.11, f32[64]{0:T(128)S(1)} %get-tuple-element.20, f32[7680]{0:T(1024)S(1)} %get-tuple-element.12, f32[64]{0:T(128)S(1)} %get-tuple-element.19, ...), kind=kOutput, calls=%fused_computation.15 | convolution fusion | flops 100531200 | bytes 3128625 | tf_op jit(solution)/shard_map/dot_general | solution.py:71
  104.6 1.9 %collective-permute-start.1 = (bf16[2,2,7680]{2,0,1:T(2,128)(2,1)S(1)}, bf16[2,2,7680]{2,0,1:T(2,128)(2,1)S(1)}, u32[]{:S(2)}, u32[]{:S(2)}) collective-permute-start(bf16[2,2,7680]{2,0,1:T(2,128)(2,1)S(1)} %collective-permute-done), channel_id=1, source_target_pairs={{0,1},{1,2},{2,3},{3,0},{4,5},{5,6},{6,7},{7,4},{8,9},{9,10},{10,1... | collective-permute-start | bytes 184328 | tf_op jit(solution)/shard_map/ppermute | solution.py:124
  106.6 7.3 %multiply_add_fusion = f32[2,49,64]{2,1,0:T(8,128)S(1)} fusion(f32[2,49,64]{2,1,0:T(8,128)S(1)} %fusion.2, f32[7680]{0:T(1024)S(1)} %get-tuple-element.11, f32[64]{0:T(128)S(1)} %get-tuple-element.20, f32[7680]{0:T(1024)S(1)} %get-tuple-element.12, f32[64]{0:T(128)S(1)} %get-tuple-element.19, f32[7680]{0:T(1024)S(1)} %get-tuple-element.10, ...), kind=kOutput, calls=%fused_computation.30 | convolution fusion | flops 100562560 | bytes 3154105 | tf_op jit(solution)/shard_map/dot_general | solution.py:68
  114.0 18.6 %all-reduce = f32[2,49,64]{1,0,2:T(2,128)S(1)} all-reduce(f32[2,49,64]{1,0,2:T(2,128)S(1)} %copy.12), channel_id=2, replica_groups=mesh['atoms'=8,'gsplit'=4] {'gsplit'}, use_global_device_ids=true, to_apply=%region_3.4.clone | all-reduce | flops 6272 | bytes 50176
  132.9 0.6 copy.13
  133.6 5.4 %collective-permute-done.2 = bf16[2,2,7680]{2,0,1:T(2,128)(2,1)S(1)} collective-permute-done((bf16[2,2,7680]{2,0,1:T(2,128)(2,1)S(1)}, bf16[2,2,7680]{2,0,1:T(2,128)(2,1)S(1)}, u32[]{:S(2)}, u32[]{:S(2)}) %collective-permute-start.2) | collective-permute-done | bytes 61472 | tf_op jit(solution)/shard_map/ppermute | solution.py:124
  139.4 14.1 %fusion.1 = f32[2,32]{1,0:T(2,128)S(1)} fusion(f32[30720]{0:T(1024)S(1)} %bitcast.69, f32[32]{0:T(128)S(1)} %get-tuple-element.22, f32[30720]{0:T(1024)S(1)} %bitcast.71, f32[32]{0:T(128)S(1)} %get-tuple-element.23, f32[30720]{0:T(1024)S(1)} %bitcast.67, f32[32]{0:T(128)S(1)} %get-tuple-element.21, ...), kind=kOutput, calls=%fused_computation.12 | convolution fusion | flops 10813440 | bytes 493320 | tf_op jit(solution)/shard_map/dot_general | solution.py:86
  153.5 14.6 %fusion.9 = f32[2,32]{1,0:T(2,128)} fusion(f32[2,32]{1,0:T(2,128)S(1)} %fusion.1, f32[30720]{0:T(1024)S(1)} %bitcast.70, f32[32]{0:T(128)S(1)} %get-tuple-element.22, f32[30720]{0:T(1024)S(1)} %bitcast.72, f32[32]{0:T(128)S(1)} %get-tuple-element.23, f32[30720]{0:T(1024)S(1)} %bitcast.68, f32[32]{0:T(128)S(1)} %get-tuple-element.21, ...), kind=kOutput, calls=%fused_computation.23 | convolution fusion | flops 10813504 | bytes 494340 | tf_op jit(solution)/shard_map/dot_general | solution.py:84
  (34 shorter events, 1.7 us)
Async XLA Ops:
  7.2 86.9 %all-reduce.3.cloned.1.call-start = ((), (), s32[]{:S(2)}) async-start(), calls=%async_computation | async-start | bytes 245760 | tf_op jit(solution)/shard_map/psum | solution.py:100
  33.1 5.4 %copy-start = (s32[3,7680]{1,0:T(4,128)S(1)}, s32[3,7680]{1,0:T(4,128)}, u32[]{:S(2)}) copy-start(s32[3,7680]{1,0:T(4,128)} %param.6) | copy-start | bytes 276484
  37.7 18.3 %copy-start.1 = (f32[3,64]{1,0:T(4,128)S(1)}, f32[3,64]{1,0:T(4,128)}, u32[]{:S(2)}) copy-start(f32[3,64]{1,0:T(4,128)} %param.8) | copy-start | bytes 2308
  37.7 18.3 %copy-start.2 = (f32[3,32]{1,0:T(4,128)S(1)}, f32[3,32]{1,0:T(4,128)}, u32[]{:S(2)}) copy-start(f32[3,32]{1,0:T(4,128)} %param.11) | copy-start | bytes 1156
  37.7 18.3 %copy-start.3 = (s32[32]{0:T(128)S(1)}, s32[32]{0:T(128)}, u32[]{:S(2)}) copy-start(s32[32]{0:T(128)} %param.10) | copy-start | bytes 388
  37.7 18.4 %copy-start.4 = (u32[32]{0:T(128)S(1)}, u32[32]{0:T(128)}, u32[]{:S(2)}) copy-start(u32[32]{0:T(128)} %constant.87) | copy-start | bytes 388
  95.5 9.2 %collective-permute-start = (bf16[2,2,7680]{2,0,1:T(2,128)(2,1)S(1)}, bf16[2,2,7680]{2,0,1:T(2,128)(2,1)S(1)}, u32[]{:S(2)}, u32[]{:S(2)}) collective-permute-start(bf16[2,2,7680]{2,0,1:T(2,128)(2,1)S(1)} %get-tuple-element.13), channel_id=1, source_target_pairs={{0,1},{1,2},{2,3},{3,0},{4,5},{5,6},{6,7},{7,4},{8,9},{9,10},{10,1... | collective-permute-start | bytes 184328 | tf_op jit(solution)/shard_map/ppermute | solution.py:124
  104.6 28.0 %collective-permute-start.1 = (bf16[2,2,7680]{2,0,1:T(2,128)(2,1)S(1)}, bf16[2,2,7680]{2,0,1:T(2,128)(2,1)S(1)}, u32[]{:S(2)}, u32[]{:S(2)}) collective-permute-start(bf16[2,2,7680]{2,0,1:T(2,128)(2,1)S(1)} %collective-permute-done), channel_id=1, source_target_pairs={{0,1},{1,2},{2,3},{3,0},{4,5},{5,6},{6,7},{7,4},{8,9},{9,10},{10,1... | collective-permute-start | bytes 184328 | tf_op jit(solution)/shard_map/ppermute | solution.py:124
  132.7 6.2 %collective-permute-start.2 = (bf16[2,2,7680]{2,0,1:T(2,128)(2,1)S(1)}, bf16[2,2,7680]{2,0,1:T(2,128)(2,1)S(1)}, u32[]{:S(2)}, u32[]{:S(2)}) collective-permute-start(bf16[2,2,7680]{2,0,1:T(2,128)(2,1)S(1)} %collective-permute-done.1), channel_id=1, source_target_pairs={{0,1},{1,2},{2,3},{3,0},{4,5},{5,6},{6,7},{7,4},{8,9},{9,10},{10,1... | collective-permute-start | bytes 184328 | tf_op jit(solution)/shard_map/ppermute | solution.py:124
Sparse Core Ops, SparseCore 0:
  38.6 55.4 all-reduce.2
